TPU v7x, 32 devices: a whole 2x2x4 slice. The times are simulated.
32 devices in a mesh: ens: 2 (over x), time: 4 (over z), chan: 4 (over y, core).
Axes of the slice: x: 2, y: 2, z: 4, core: 2. Of those that a mesh axis runs over, the one named last changes fastest.
Arguments:
- decay_rate: float32 [4, 4096, 1024], P('ens', 'time', 'chan'), parts along dimension 0, may hold values from 0.2 to 2
- drive_in: bfloat16 [4, 4096, 1024], P('ens', 'time', 'chan'), parts along dimension 0, may hold values from -6 to 6
- gate_in: bfloat16 [4, 4096, 1024], P('ens', 'time', 'chan'), parts along dimension 0, may hold values from -6 to 6
- norm_gain: float32 [2048], P(('ens', 'chan')), parts along dimension 0, may hold values from 0.25 to 1.75
Outputs:
- mixed_out: bfloat16 [4, 4096, 1024], P('ens', 'time', 'chan'), parts along dimension 0
There are 2 independent parts, one for each index of `ens`. A program takes and returns all parts, laid end to end along the dimension named above; each array names one. Nothing has to cross between parts.
All inputs are finite; a program needn't handle non-finite values.
Results may differ from a plain program's by a relative error of at most 0.001.
Values sent between devices are 32-bit elements.
A program may use at most 64 MiB of HBM per device.

v0:
```python
import jax
import jax.numpy as jnp
from jax import lax
from jax.sharding import PartitionSpec as P


def prefix(value, axis, combine, identity, reverse):
    devices, position = lax.axis_size(axis), lax.axis_index(axis)
    everything = jax.tree.map(lambda part: lax.all_gather(part, axis), value)
    start = jax.tree.map(
        lambda part, zero: jnp.broadcast_to(jnp.asarray(zero, part.dtype), part.shape),
        value,
        identity,
    )

    def hop(k, before):
        at = devices - 1 - k if reverse else k
        reached = at > position if reverse else at < position
        new = combine(before, jax.tree.map(lambda part: part[at], everything))
        return jax.tree.map(lambda a, b: jnp.where(reached, a, b), new, before)

    return lax.fori_loop(0, devices, hop, start)


def join_pair(earlier, later):
    return (earlier[0] * later[0], later[0] * earlier[1] + later[1])


def local(decay_rate, drive_in, gate_in, norm_gain):
    total_length = decay_rate.shape[1] * lax.axis_size("time")
    keep = jnp.exp(-decay_rate / total_length)
    push = drive_in.astype(jnp.float32) * total_length ** (-0.5)
    product, forward = lax.associative_scan(join_pair, (keep, push), axis=1)
    entering_forward = prefix(
        (product[:, -1], forward[:, -1]),
        "time",
        join_pair,
        (jnp.ones_like(keep[:, 0]), jnp.zeros_like(push[:, 0])),
        False,
    )
    forward = forward + product * entering_forward[1][:, None]
    product, backward = lax.associative_scan(join_pair, (keep, push), axis=1, reverse=True)
    entering_backward = prefix(
        (product[:, 0], backward[:, 0]),
        "time",
        join_pair,
        (jnp.ones_like(keep[:, 0]), jnp.zeros_like(push[:, 0])),
        True,
    )
    backward = backward + product * entering_backward[1][:, None]
    states = forward + backward
    gated = states * jax.nn.silu(gate_in.astype(jnp.float32))
    power = lax.psum(jnp.sum(gated * gated, axis=-1, keepdims=True), "chan") / (
        gated.shape[-1] * lax.axis_size("chan")
    )
    mixed_out = (gated * lax.rsqrt(power + 1e-06) * norm_gain).astype(jnp.bfloat16)
    return mixed_out


def solution(mesh):
    in_specs = (
        P("ens", "time", "chan"),
        P("ens", "time", "chan"),
        P("ens", "time", "chan"),
        P(("ens", "chan")),
    )
    out_specs = P("ens", "time", "chan")
    return jax.shard_map(local, mesh=mesh, in_specs=in_specs, out_specs=out_specs, check_vma=False)
```

profile of v0, /device:TPU:0, one launch (start us, length us, event | category | flops | bytes accessed | tf_op | source)
XLA Modules:
  0.0 273.2 jit_solution(8357931440608761692)
XLA Ops:
  0.0 1.9 multiply_exponential_fusion
  1.9 1.2 slice.606
  3.1 3.6 %slice.602 = f32[2,512,256]{2,1,0:T(8,128)} slice(f32[2,1024,256]{2,1,0:T(8,128)S(1)} %multiply_exponential_fusion), slice={[0:2:1], [1:1024:2], [0:256:1]} | slice | bytes 2097152 | tf_op jit(solution)/shard_map/slice | solution.py:33
  6.7 8.9 %slice.703 = f32[2,512,256]{2,1,0:T(8,128)} reverse(f32[2,512,256]{2,1,0:T(8,128)} %slice.602), dimensions={1} | reverse | bytes 2097152 | tf_op jit(solution)/shard_map/slice | solution.py:42
  15.6 5.2 %slice.699 = f32[2,512,256]{2,1,0:T(8,128)} reverse(f32[2,512,256]{2,1,0:T(8,128)S(1)} %slice.606), dimensions={1} | reverse | bytes 2097152 | tf_op jit(solution)/shard_map/slice | solution.py:42
  20.7 3.6 %slice.697 = f32[2,511,256]{2,1,0:T(8,128)} slice(f32[2,1024,256]{2,1,0:T(8,128)S(1)} %multiply_exponential_fusion), slice={[0:2:1], [1:1022:2], [0:256:1]} | slice | bytes 2093056 | tf_op jit(solution)/shard_map/slice | solution.py:42
  24.3 3.6 %slice.601 = f32[2,511,256]{2,1,0:T(8,128)} slice(f32[2,1024,256]{2,1,0:T(8,128)S(1)} %multiply_exponential_fusion), slice={[0:2:1], [2:1024:2], [0:256:1]} | slice | bytes 2093056 | tf_op jit(solution)/shard_map/slice | solution.py:33
  27.9 9.1 %slice.698 = f32[2,511,256]{2,1,0:T(8,128)} reverse(f32[2,511,256]{2,1,0:T(8,128)} %slice.697), dimensions={1} | reverse | bytes 2093056 | tf_op jit(solution)/shard_map/slice | solution.py:42
  37.0 1.4 broadcast_multiply_fusion.1
  38.4 3.7 %slice.674 = f32[2,511,256]{2,1,0:T(8,128)} slice(f32[2,1024,256]{2,1,0:T(8,128)S(1)} %broadcast_multiply_fusion.1), slice={[0:2:1], [2:1024:2], [0:256:1]} | slice | bytes 2093056 | tf_op jit(solution)/shard_map/slice | solution.py:33
  42.1 3.6 %slice.604 = f32[2,512,256]{2,1,0:T(8,128)} slice(f32[2,1024,256]{2,1,0:T(8,128)S(1)} %broadcast_multiply_fusion.1), slice={[0:2:1], [1:1024:2], [0:256:1]} | slice | bytes 2097152 | tf_op jit(solution)/shard_map/slice | solution.py:33
  45.7 3.6 %slice.603 = f32[2,512,256]{2,1,0:T(8,128)} slice(f32[2,1024,256]{2,1,0:T(8,128)S(1)} %broadcast_multiply_fusion.1), slice={[0:2:1], [0:1023:2], [0:256:1]} | slice | bytes 2097152 | tf_op jit(solution)/shard_map/slice | solution.py:33
  49.3 2.1 multiply_add_fusion.1
  51.5 2.2 slice.672
  53.7 2.2 slice.610
  55.8 2.2 slice.609
  58.0 2.2 slice.612
  60.2 2.1 slice.608
  62.3 1.3 multiply_add_fusion.3
  69.7 0.9 add.521
  70.6 0.9 add.509
  72.0 1.2 pad.261
  73.2 2.9 %pad.281 = f32[2,512,256]{2,1,0:T(8,128)} pad(f32[2,256,256]{2,1,0:T(8,128)} %add.521, f32[]{:T(128)} %constant.80.clone.1), padding=0_0_0x1_0_1x0_0_0 | pad | bytes 1572868 | tf_op jit(solution)/shard_map/pad | solution.py:33
  76.1 2.3 fusion.7
  78.5 1.1 add.522
  79.6 1.1 add.511
  80.7 1.1 pad_maximum_fusion
  82.3 5.6 %pad.262 = f32[2,1024,256]{2,1,0:T(8,128)} pad(f32[2,512,256]{2,1,0:T(8,128)} %pad_maximum_fusion, f32[]{:T(128)} %constant.80.clone.1), padding=0_0_0x0_1_1x0_0_0 | pad | bytes 3145732 | tf_op jit(solution)/shard_map/pad | solution.py:33
  87.9 3.5 %pad.263 = f32[2,1024,256]{2,1,0:T(8,128)} pad(f32[2,512,256]{2,1,0:T(8,128)S(1)} %copy-done.6, f32[]{:T(128)} %constant.80.clone.1), padding=0_0_0x1_0_1x0_0_0 | pad | bytes 3145732 | tf_op jit(solution)/shard_map/pad | solution.py:33
  91.4 0.8 slice_add_fusion.4
  92.3 14.8 %all-gather.1 = f32[8,1,256]{2,1,0:T(1,128)S(1)} all-gather(f32[2,1,256]{2,1,0:T(1,128)S(1)} %slice_add_fusion.4), channel_id=3, replica_groups=mesh['ens'=2,'time'=4,'chan'=4] {'time'}, dimensions={0}, use_global_device_ids=true | all-gather | bytes 10240 | tf_op jit(solution)/shard_map/all_gather | solution.py:9
  107.1 5.3 %pad.283 = f32[2,1024,256]{2,1,0:T(8,128)} pad(f32[2,512,256]{2,1,0:T(8,128)} %add.522, f32[]{:T(128)} %constant.80.clone.1), padding=0_0_0x1_0_1x0_0_0 | pad | bytes 3145732 | tf_op jit(solution)/shard_map/pad | solution.py:33
  112.4 0.7 slice_add_fusion.5
  113.1 13.3 %all-gather = f32[8,1,256]{2,1,0:T(1,128)S(1)} all-gather(f32[2,1,256]{2,1,0:T(1,128)S(1)} %slice_add_fusion.5), channel_id=2, replica_groups=mesh['ens'=2,'time'=4,'chan'=4] {'time'}, dimensions={0}, use_global_device_ids=true | all-gather | bytes 10240 | tf_op jit(solution)/shard_map/all_gather | solution.py:9
  126.6 10.5 %reverse.9 = f32[2,1024,256]{2,1,0:T(8,128)} reverse(bf16[2,1024,256]{2,1,0:T(8,128)(2,1)S(1)} %copy-done.4), dimensions={1} | reverse | bytes 3145728 | tf_op jit(solution)/shard_map/reverse
  137.1 1.7 broadcast_multiply_fusion
  138.8 3.7 %slice.771 = f32[2,511,256]{2,1,0:T(8,128)} slice(f32[2,1024,256]{2,1,0:T(8,128)S(1)} %broadcast_multiply_fusion), slice={[0:2:1], [2:1024:2], [0:256:1]} | slice | bytes 2093056 | tf_op jit(solution)/shard_map/slice | solution.py:42
  142.5 3.6 %slice.701 = f32[2,512,256]{2,1,0:T(8,128)} slice(f32[2,1024,256]{2,1,0:T(8,128)S(1)} %broadcast_multiply_fusion), slice={[0:2:1], [1:1024:2], [0:256:1]} | slice | bytes 2097152 | tf_op jit(solution)/shard_map/slice | solution.py:42
  146.1 3.6 %slice.700 = f32[2,512,256]{2,1,0:T(8,128)} slice(f32[2,1024,256]{2,1,0:T(8,128)S(1)} %broadcast_multiply_fusion), slice={[0:2:1], [0:1023:2], [0:256:1]} | slice | bytes 2097152 | tf_op jit(solution)/shard_map/slice | solution.py:42
  149.7 2.1 fusion.32
  153.2 2.2 slice.704
  155.4 2.2 slice.769
  164.7 0.9 add.549
  165.5 0.9 add.561
  166.9 1.2 pad.321
  168.1 2.9 %pad.301 = f32[2,512,256]{2,1,0:T(8,128)} pad(f32[2,256,256]{2,1,0:T(8,128)} %add.549, f32[]{:T(128)} %constant.80.clone.1), padding=0_0_0x1_0_1x0_0_0 | pad | bytes 1572868 | tf_op jit(solution)/shard_map/pad | solution.py:42
  171.1 2.4 add_multiply_fusion
  173.4 1.1 add.551
  174.5 1.1 add.562
  175.7 1.1 pad_maximum_fusion.3
  177.2 5.4 %pad.322 = f32[2,1024,256]{2,1,0:T(8,128)} pad(f32[2,512,256]{2,1,0:T(8,128)} %pad_maximum_fusion.3, f32[]{:T(128)} %constant.80.clone.1), padding=0_0_0x0_1_1x0_0_0 | pad | bytes 3145732 | tf_op jit(solution)/shard_map/pad | solution.py:42
  182.7 3.5 %pad.323 = f32[2,1024,256]{2,1,0:T(8,128)} pad(f32[2,512,256]{2,1,0:T(8,128)S(1)} %copy-done.7, f32[]{:T(128)} %constant.80.clone.1), padding=0_0_0x1_0_1x0_0_0 | pad | bytes 3145732 | tf_op jit(solution)/shard_map/pad | solution.py:42
  186.2 0.7 slice_add_fusion.1
  186.9 3.9 %add.563 = f32[2,1024,256]{2,1,0:T(8,128)} add(f32[2,1024,256]{2,1,0:T(8,128)} %pad.322, f32[2,1024,256]{2,1,0:T(8,128)} %pad.323) | non-fusion elementwise | flops 524288 | bytes 6291456 | tf_op jit(solution)/shard_map/add | solution.py:42
  190.8 16.7 %rev.12 = f32[2,1024,256]{2,1,0:T(8,128)} reverse(f32[2,1024,256]{2,1,0:T(8,128)} %add.563), dimensions={1} | reverse | bytes 4194304 | tf_op jit(solution)/shard_map/rev | solution.py:42
  207.5 13.0 %all-gather.2 = f32[8,1,256]{2,1,0:T(1,128)S(1)} all-gather(f32[2,1,256]{2,1,0:T(1,128)S(1)} %slice_add_fusion.1), channel_id=4, replica_groups=mesh['ens'=2,'time'=4,'chan'=4] {'time'}, dimensions={0}, use_global_device_ids=true | all-gather | bytes 10240 | tf_op jit(solution)/shard_map/all_gather | solution.py:9
  220.6 3.4 %pad.303 = f32[2,1024,256]{2,1,0:T(8,128)} pad(f32[2,512,256]{2,1,0:T(8,128)S(1)} %copy-done.5, f32[]{:T(128)} %constant.80.clone.1), padding=0_0_0x1_0_1x0_0_0 | pad | bytes 3145732 | tf_op jit(solution)/shard_map/pad | solution.py:42
  224.0 0.7 slice_add_fusion
  224.7 3.2 %add.553 = f32[2,1024,256]{2,1,0:T(8,128)} add(f32[2,1024,256]{2,1,0:T(8,128)S(1)} %pad.302, f32[2,1024,256]{2,1,0:T(8,128)} %pad.303) | non-fusion elementwise | flops 524288 | bytes 6291456 | tf_op jit(solution)/shard_map/add | solution.py:42
  227.9 16.8 %rev.11 = f32[2,1024,256]{2,1,0:T(8,128)} reverse(f32[2,1024,256]{2,1,0:T(8,128)} %add.553), dimensions={1} | reverse | bytes 4194304 | tf_op jit(solution)/shard_map/rev | solution.py:42
  244.6 13.0 %all-gather.3 = f32[8,1,256]{2,1,0:T(1,128)S(1)} all-gather(f32[2,1,256]{2,1,0:T(1,128)S(1)} %slice_add_fusion), channel_id=5, replica_groups=mesh['ens'=2,'time'=4,'chan'=4] {'time'}, dimensions={0}, use_global_device_ids=true | all-gather | bytes 10240 | tf_op jit(solution)/shard_map/all_gather | solution.py:9
  257.9 6.6 %multiply_reduce_fusion = (f32[2,1024]{1,0:T(2,128)S(1)}, f32[2,1024,256]{2,1,0:T(8,128)}) fusion(bf16[2,1024,256]{2,1,0:T(8,128)(2,1)S(1)} %copy-done.14, f32[2,1024,256]{2,1,0:T(8,128)} %rev.11, f32[2,1024,256]{2,1,0:T(8,128)} %rev.12, f32[2,256]{1,0:T(2,128)S(1)} %get-tuple-element.232, f32[2,256]{1,0:T(2,128)S(1)} %get-tuple-element.231, ...), kind=kLoop, calls=%fused_computation.13 | loop fusion | flops 7862272 | bytes 15740928 | tf_op jit(solution)/shard_map/reduce_sum | solution.py:53
  264.5 5.7 %psum.7 = f32[2,1024,1]{1,0,2:T(2,128)S(1)} all-reduce(f32[2,1024,1]{1,0,2:T(2,128)S(1)} %bitcast.51), channel_id=1, replica_groups=mesh['ens'=2,'time'=4,'chan'=4] {'chan'}, use_global_device_ids=true, to_apply=%region_5.6 | all-reduce | flops 2048 | bytes 16384 | tf_op jit(solution)/shard_map/psum | solution.py:53
  270.3 2.9 %multiply_convert_fusion = bf16[2,1024,256]{2,1,0:T(8,128)(2,1)} fusion(f32[2,1024,256]{2,1,0:T(8,128)} %get-tuple-element.290, f32[256]{0:T(256)S(1)} %copy-done.15, f32[2,1024]{1,0:T(2,128)S(1)} %rsqrt_bitcast_fusion), kind=kLoop, calls=%fused_computation.12 | loop fusion | flops 1572864 | bytes 3154944 | tf_op jit(solution)/shard_map/convert_element_type | solution.py:56
  (322 shorter events, 15.7 us)
Async XLA Ops:
  58.0 4.3 %copy-start.9 = (f32[2,256,256]{2,1,0:T(8,128)S(1)}, f32[2,256,256]{2,1,0:T(8,128)}, u32[]{:S(2)}) copy-start(f32[2,256,256]{2,1,0:T(8,128)} %slice.610) | copy-start | bytes 1572868
  58.0 4.3 %copy-start.10 = (f32[2,256,256]{2,1,0:T(8,128)S(1)}, f32[2,256,256]{2,1,0:T(8,128)}, u32[]{:S(2)}) copy-start(f32[2,256,256]{2,1,0:T(8,128)} %slice.609) | copy-start | bytes 1572868
  68.5 1.0 copy-start.11
  76.1 2.4 copy-start
  82.3 30.1 %copy-start.2 = (f32[2,1024,256]{2,1,0:T(8,128)}, f32[2,1024,256]{2,1,0:T(8,128)S(1)}, u32[]{:S(2)}) copy-start(f32[2,1024,256]{2,1,0:T(8,128)S(1)} %pad.282) | copy-start | bytes 6291460
  82.3 5.6 %copy-start.6 = (f32[2,512,256]{2,1,0:T(8,128)S(1)}, f32[2,512,256]{2,1,0:T(8,128)}, u32[]{:S(2)}) copy-start(f32[2,512,256]{2,1,0:T(8,128)} %add.511) | copy-start | bytes 3145732
  91.4 35.2 %copy-start.4 = (bf16[2,1024,256]{2,1,0:T(8,128)(2,1)S(1)}, bf16[2,1024,256]{2,1,0:T(8,128)(2,1)}, u32[]{:S(2)}) copy-start(bf16[2,1024,256]{2,1,0:T(8,128)(2,1)} %param.9) | copy-start | bytes 3145732
  142.5 7.2 %copy-start.8 = (f32[2,512,256]{2,1,0:T(8,128)S(1)}, f32[2,512,256]{2,1,0:T(8,128)}, u32[]{:S(2)}) copy-start(f32[2,512,256]{2,1,0:T(8,128)} %slice.703) | copy-start | bytes 3145732
  163.2 1.0 copy-start.12
  163.3 1.2 copy-start.13
  171.1 2.4 copy-start.1
  177.2 5.4 %copy-start.7 = (f32[2,512,256]{2,1,0:T(8,128)S(1)}, f32[2,512,256]{2,1,0:T(8,128)}, u32[]{:S(2)}) copy-start(f32[2,512,256]{2,1,0:T(8,128)} %add.562) | copy-start | bytes 3145732
  190.8 29.8 %copy-start.5 = (f32[2,512,256]{2,1,0:T(8,128)S(1)}, f32[2,512,256]{2,1,0:T(8,128)}, u32[]{:S(2)}) copy-start(f32[2,512,256]{2,1,0:T(8,128)} %add.551) | copy-start | bytes 3145732
  227.9 30.0 %copy-start.3 = (f32[2,1024,256]{2,1,0:T(8,128)S(1)}, f32[2,1024,256]{2,1,0:T(8,128)}, u32[]{:S(2)}) copy-start(f32[2,1024,256]{2,1,0:T(8,128)} %copy-done.2) | copy-start | bytes 6291460
  227.9 30.0 %copy-start.14 = (bf16[2,1024,256]{2,1,0:T(8,128)(2,1)S(1)}, bf16[2,1024,256]{2,1,0:T(8,128)(2,1)}, u32[]{:S(2)}) copy-start(bf16[2,1024,256]{2,1,0:T(8,128)(2,1)} %param.10) | copy-start | bytes 3145732
  257.9 12.3 %copy-start.15 = (f32[256]{0:T(256)S(1)}, f32[256]{0:T(256)}, u32[]{:S(2)}) copy-start(f32[256]{0:T(256)} %param.11) | copy-start | bytes 3076
where the time goes:
time: 277 us; the launch traced here: 273 us
  local copies, waits for them, and re-layouts  164 us (59%)
  blocking collectives  59.8 us (22%)
  other arithmetic  47.4 us (17%)
    all_gather x4, blocking collectives, prefix(): everything = jax.tree.map(lambda part: lax.all_gather(part, axis), value)  54.1 us
    slice x68, local copies, waits for them, and re-layouts, local(): lax.associative_scan(join_pair, (keep, push), axis=1, reverse=True)  46.7 us
    rev x2, local copies, waits for them, and re-layouts, local(): lax.associative_scan(join_pair, (keep, push), axis=1, reverse=True)  33.5 us
    slice x68, local copies, waits for them, and re-layouts, local(): product, forward = lax.associative_scan(join_pair, (keep, push), axis=1)  32.8 us
    pad x36, local copies, waits for them, and re-layouts, local(): product, forward = lax.associative_scan(join_pair, (keep, push), axis=1)  20.7 us
    pad x36, local copies, waits for them, and re-layouts, local(): lax.associative_scan(join_pair, (keep, push), axis=1, reverse=True)  18.6 us
    add x21, other arithmetic, local(): lax.associative_scan(join_pair, (keep, push), axis=1, reverse=True)  12.6 us
    another operation x1, local copies, waits for them, and re-layouts  10.5 us

commit v1 on v0

v1 whole, which is shorter than its diff:
```python
import functools

import jax
import jax.numpy as jnp
from jax import lax
from jax.experimental import pallas as pl
from jax.experimental.pallas import tpu as pltpu
from jax.sharding import PartitionSpec as P

MESH = pl.DeviceIdType.MESH
LANES = 128


def split(value):
    high = value.astype(jnp.bfloat16)
    return high, (value - high.astype(jnp.float32)).astype(jnp.bfloat16)


def sums(triangle, value):
    high, low = split(value)
    return jnp.dot(triangle, high, preferred_element_type=jnp.float32) + jnp.dot(
        triangle, low, preferred_element_type=jnp.float32
    )


def kernel(
    batch, span, times, chans, length,
    decay_hbm, drive_hbm, gate_hbm, gain_ref, out_ref,
    base, drive, gate, fall, rise, back,
    stats, entering, mine, others, column, power, powers,
    load_sem, send_sem, recv_sem, power_send_sem, power_recv_sem,
):
    chunks, size, channels = base.shape
    time, chan = lax.axis_index("time"), lax.axis_index("chan")

    def load(which, c):
        source, target = ((decay_hbm, base), (drive_hbm, drive), (gate_hbm, gate))[which]
        return pltpu.make_async_copy(source.at[c], target.at[c], load_sem.at[which, c])

    for c in range(chunks):
        load(0, c).start()
        load(1, c).start()
    for c in range(chunks):
        load(2, c).start()

    barrier = pltpu.get_barrier_semaphore()
    for d in range(1, times):
        pl.semaphore_signal(barrier, inc=1, device_id={"time": lax.rem(time + d, times)}, device_id_type=MESH)
    for d in range(1, chans):
        pl.semaphore_signal(barrier, inc=1, device_id={"chan": lax.rem(chan + d, chans)}, device_id_type=MESH)

    row = lax.broadcasted_iota(jnp.int32, (size, size), 0)
    col = lax.broadcasted_iota(jnp.int32, (size, size), 1)
    lower = jnp.where(row >= col, 1.0, 0.0).astype(jnp.bfloat16)
    upper = jnp.where(row <= col, 1.0, 0.0).astype(jnp.bfloat16)

    def scan(c, _):
        load(0, c).wait()
        load(1, c).wait()
        rate = base[c] * (1.0 / length)
        total = sums(lower, rate)
        push = drive[c].astype(jnp.float32) * length ** (-0.5)
        up, down = jnp.exp(total), jnp.exp(-total)
        fall[c] = down
        rise[c] = up * jnp.exp(-rate)
        ahead = sums(lower, up * push)
        behind = sums(upper, down * jnp.exp(rate) * push)
        base[c] = ahead
        back[c] = behind
        stats[c, 0:1] = down[size - 1 :]
        stats[c, 1:2] = down[size - 1 :] * ahead[size - 1 :]
        stats[c, 2:3] = behind[0:1]
        return _

    lax.fori_loop(0, chunks, scan, 0)

    mine[...] = jnp.zeros(mine.shape, jnp.float32)
    for b in range(batch):
        product = jnp.ones((1, channels), jnp.float32)
        forward = jnp.zeros((1, channels), jnp.float32)
        backward = jnp.zeros((1, channels), jnp.float32)
        for j in range(span):
            keep = stats[b * span + j, 0:1]
            product = product * keep
            forward = keep * forward + stats[b * span + j, 1:2]
        for j in reversed(range(span)):
            backward = stats[b * span + j, 0:1] * backward + stats[b * span + j, 2:3]
        mine[3 * b : 3 * b + 1] = product
        mine[3 * b + 1 : 3 * b + 2] = forward
        mine[3 * b + 2 : 3 * b + 3] = backward

    pl.semaphore_wait(barrier, times + chans - 2)

    def exchange(d):
        return pltpu.make_async_remote_copy(
            src_ref=mine, dst_ref=others.at[d - 1],
            send_sem=send_sem.at[d - 1], recv_sem=recv_sem.at[d - 1],
            device_id={"time": lax.rem(time + d, times)}, device_id_type=MESH,
        )

    for d in range(1, times):
        exchange(d).start()

    def weigh(c, _):
        load(2, c).wait()
        value = gate[c].astype(jnp.float32)
        gated = 0.5 * value * (1.0 + jnp.tanh(0.5 * value))
        ahead, behind = fall[c] * gated, rise[c] * gated
        base[c] = ahead * base[c] + behind * back[c]
        fall[c] = ahead
        rise[c] = behind
        return _

    lax.fori_loop(0, chunks, weigh, 0)

    for d in range(1, times):
        exchange(d).wait()

    for b in range(batch):
        forward = jnp.zeros((1, channels), jnp.float32)
        backward = jnp.zeros((1, channels), jnp.float32)
        for d in reversed(range(1, times)):
            new = others[d - 1, 3 * b : 3 * b + 1] * forward + others[d - 1, 3 * b + 1 : 3 * b + 2]
            forward = jnp.where(time >= d, new, forward)
            slot = times - d - 1
            new = others[slot, 3 * b : 3 * b + 1] * backward + others[slot, 3 * b + 2 : 3 * b + 3]
            backward = jnp.where(time + d < times, new, backward)
        for j in range(span):
            entering[b * span + j, 0:1] = forward
            forward = stats[b * span + j, 0:1] * forward + stats[b * span + j, 1:2]
        for j in reversed(range(span)):
            backward = stats[b * span + j, 0:1] * backward
            entering[b * span + j, 1:2] = backward
            backward = backward + stats[b * span + j, 2:3]

    lane = lax.broadcasted_iota(jnp.int32, (size, LANES), 1)
    column[...] = jnp.zeros((size, LANES), jnp.float32)

    def join(c, _):
        gated = base[c] + fall[c] * entering[c, 0:1] + rise[c] * entering[c, 1:2]
        base[c] = gated
        squares = jnp.sum(gated * gated, axis=-1, keepdims=True)
        column[...] = jnp.where(lane == c, squares, column[...])
        return _

    lax.fori_loop(0, chunks, join, 0)
    power[...] = jnp.transpose(column[...])[: power.shape[0]]

    def spread(d):
        return pltpu.make_async_remote_copy(
            src_ref=power, dst_ref=powers.at[d - 1],
            send_sem=power_send_sem.at[d - 1], recv_sem=power_recv_sem.at[d - 1],
            device_id={"chan": lax.rem(chan + d, chans)}, device_id_type=MESH,
        )

    for d in range(1, chans):
        spread(d).start()
    for d in range(1, chans):
        spread(d).wait()
    total = power[...]
    for d in range(1, chans):
        total = total + powers[d - 1]
    scale = lax.rsqrt(total / (channels * chans) + 1e-06)
    scale = jnp.concatenate([scale, jnp.zeros((LANES - scale.shape[0], size), jnp.float32)], axis=0)
    column[...] = jnp.transpose(scale)
    gain = gain_ref[...]
    for c in range(chunks):
        out_ref[c] = (base[c] * column[:, c : c + 1] * gain).astype(jnp.bfloat16)


def solution(mesh):
    times, chans = mesh.shape["time"], mesh.shape["chan"]

    def local(decay_rate, drive_in, gate_in, norm_gain):
        batch, positions, channels = decay_rate.shape
        size = min(256, positions)
        span = positions // size
        chunks = batch * span
        rows = -(-3 * batch // 8) * 8
        power_rows = -(-chunks // 8) * 8
        whole = (chunks, size, channels)
        out = pl.pallas_call(
            functools.partial(kernel, batch, span, times, chans, positions * times),
            out_shape=pltpu.VMEM(whole, jnp.bfloat16),
            in_specs=[pl.BlockSpec(memory_space=pl.ANY)] * 3 + [pl.BlockSpec(memory_space=pltpu.VMEM)],
            out_specs=pl.BlockSpec(memory_space=pltpu.VMEM),
            scratch_shapes=[
                pltpu.VMEM(whole, jnp.float32),
                pltpu.VMEM(whole, jnp.bfloat16),
                pltpu.VMEM(whole, jnp.bfloat16),
                pltpu.VMEM(whole, jnp.float32),
                pltpu.VMEM(whole, jnp.float32),
                pltpu.VMEM(whole, jnp.float32),
                pltpu.VMEM((chunks, 8, channels), jnp.float32),
                pltpu.VMEM((chunks, 8, channels), jnp.float32),
                pltpu.VMEM((rows, channels), jnp.float32),
                pltpu.VMEM((times - 1, rows, channels), jnp.float32),
                pltpu.VMEM((size, LANES), jnp.float32),
                pltpu.VMEM((power_rows, size), jnp.float32),
                pltpu.VMEM((chans - 1, power_rows, size), jnp.float32),
                pltpu.SemaphoreType.DMA((3, chunks)),
                pltpu.SemaphoreType.DMA((times - 1,)),
                pltpu.SemaphoreType.DMA((times - 1,)),
                pltpu.SemaphoreType.DMA((chans - 1,)),
                pltpu.SemaphoreType.DMA((chans - 1,)),
            ],
            compiler_params=pltpu.CompilerParams(
                collective_id=0, has_side_effects=True, vmem_limit_bytes=60 * 1024 * 1024
            ),
        )(
            decay_rate.reshape(whole),
            drive_in.reshape(whole),
            gate_in.reshape(whole),
            norm_gain.reshape(1, channels),
        )
        return out.reshape(decay_rate.shape)

    in_specs = (
        P("ens", "time", "chan"),
        P("ens", "time", "chan"),
        P("ens", "time", "chan"),
        P(("ens", "chan")),
    )
    return jax.shard_map(
        local, mesh=mesh, in_specs=in_specs, out_specs=P("ens", "time", "chan"), check_vma=False
    )
```

time: 277 us -> 19.7 us (0.07); the launches traced: 273 us -> 19.5 us
  local copies, waits for them, and re-layouts: 164 us -> 0.97 us
  blocking collectives: 59.8 us -> 0 us
  other arithmetic: 47.4 us -> 0 us
  Pallas kernels: 0 us -> 18.5 us
    slice x136 -> x0, local copies, waits for them, and re-layouts: 79.4 us -> none  [the longest x68 46.7 us: local(): lax.associative_scan(join_pair, (keep, push), axis=1, reverse=True)]
    all_gather x4 -> x0, blocking collectives: 54.1 us -> none  [prefix(): everything = jax.tree.map(lambda part: lax.all_gather(part, axis), value)]
    pad x72 -> x0, local copies, waits for them, and re-layouts: 39.3 us -> none  [the longest x36 20.7 us: local(): product, forward = lax.associative_scan(join_pair, (keep, push), axis=1)]
    rev x2 -> x0, local copies, waits for them, and re-layouts: 33.5 us -> none  [local(): lax.associative_scan(join_pair, (keep, push), axis=1, reverse=True)]
    add x58 -> x0, other arithmetic: 24.7 us -> none  [the longest x21 12.6 us: local(): lax.associative_scan(join_pair, (keep, push), axis=1, reverse=True)]
    pallas_call x0 -> x1, Pallas kernels: none -> 18.5 us  [local(): pl.pallas_call(functools.partial(kernel, batch, span, times, chans, posit...]
    another operation x1 -> x0, local copies, waits for them, and re-layouts: 10.5 us -> none
    mul x19 -> x0, other arithmetic: 6.63 us -> none  [the longest x17 5.23 us: join_pair(): return (earlier[0] * later[0], later[0] * earlier[1] + later[1])]
where the time goes in v1:
time: 19.7 us; the launch traced here: 19.5 us
  Pallas kernels  18.5 us (94%)
  local copies, waits for them, and re-layouts  0.97 us (5%)
    pallas_call x1, Pallas kernels, local(): pl.pallas_call(functools.partial(kernel, batch, span, times, chans, posit...  18.5 us
    unnamed x1, local copies, waits for them, and re-layouts  0.97 us

profile of v1, /device:TPU:0, one launch (start us, length us, event | category | flops | bytes accessed | tf_op | source)
XLA Modules:
  0.0 19.5 jit_solution(11763650551518366267)
XLA Ops:
  0.0 18.5 %shard_map.46 = bf16[8,256,256]{2,1,0:T(8,128)(2,1)S(1)} custom-call(f32[8,256,256]{2,1,0:T(8,128)} %bitcast.6, bf16[8,256,256]{2,1,0:T(8,128)(2,1)} %bitcast.7, bf16[8,256,256]{2,1,0:T(8,128)(2,1)} %bitcast.8, f32[1,256]{1,0:T(1,128)} %bitcast.9), custom_call_target="tpu_custom_call" | custom-call | tf_op jit(solution)/shard_map/pallas_call | solution.py:182
  18.5 1.0 %copy.6 = bf16[2,1024,256]{2,1,0:T(8,128)(2,1)} copy(bf16[2,1024,256]{2,1,0:T(8,128)(2,1)S(1)} %bitcast.5) | data formatting | bytes 2097152

commit v2 on v1

--- a/solution.py
+++ b/solution.py
@@ -1,4 +1,5 @@
 import functools
+import math
 
 import jax
 import jax.numpy as jnp
@@ -9,6 +10,18 @@
 
 MESH = pl.DeviceIdType.MESH
 LANES = 128
+GROUP = 4
+
+
+def steps(chunks, body):
+    group = GROUP if chunks % GROUP == 0 else 1
+
+    def step(i, carry):
+        for k in range(group):
+            body(i * group + k)
+        return carry
+
+    lax.fori_loop(0, chunks // group, step, 0)
 
 
 def split(value):
@@ -54,25 +67,25 @@
     lower = jnp.where(row >= col, 1.0, 0.0).astype(jnp.bfloat16)
     upper = jnp.where(row <= col, 1.0, 0.0).astype(jnp.bfloat16)
 
-    def scan(c, _):
+    def scan(c):
         load(0, c).wait()
         load(1, c).wait()
-        rate = base[c] * (1.0 / length)
+        rate = base[c] * (math.log2(math.e) / length)
         total = sums(lower, rate)
         push = drive[c].astype(jnp.float32) * length ** (-0.5)
-        up, down = jnp.exp(total), jnp.exp(-total)
+        before = total - rate
+        down = jnp.exp2(-total)
         fall[c] = down
-        rise[c] = up * jnp.exp(-rate)
-        ahead = sums(lower, up * push)
-        behind = sums(upper, down * jnp.exp(rate) * push)
+        rise[c] = jnp.exp2(before)
+        ahead = sums(lower, jnp.exp2(total) * push)
+        behind = sums(upper, jnp.exp2(-before) * push)
         base[c] = ahead
         back[c] = behind
         stats[c, 0:1] = down[size - 1 :]
         stats[c, 1:2] = down[size - 1 :] * ahead[size - 1 :]
         stats[c, 2:3] = behind[0:1]
-        return _
-
-    lax.fori_loop(0, chunks, scan, 0)
+
+    steps(chunks, scan)
 
     mine[...] = jnp.zeros(mine.shape, jnp.float32)
     for b in range(batch):
@@ -101,7 +114,7 @@
     for d in range(1, times):
         exchange(d).start()
 
-    def weigh(c, _):
+    def weigh(c):
         load(2, c).wait()
         value = gate[c].astype(jnp.float32)
         gated = 0.5 * value * (1.0 + jnp.tanh(0.5 * value))
@@ -109,9 +122,8 @@
         base[c] = ahead * base[c] + behind * back[c]
         fall[c] = ahead
         rise[c] = behind
-        return _
-
-    lax.fori_loop(0, chunks, weigh, 0)
+
+    steps(chunks, weigh)
 
     for d in range(1, times):
         exchange(d).wait()
@@ -136,14 +148,13 @@
     lane = lax.broadcasted_iota(jnp.int32, (size, LANES), 1)
     column[...] = jnp.zeros((size, LANES), jnp.float32)
 
-    def join(c, _):
+    def join(c):
         gated = base[c] + fall[c] * entering[c, 0:1] + rise[c] * entering[c, 1:2]
         base[c] = gated
         squares = jnp.sum(gated * gated, axis=-1, keepdims=True)
         column[...] = jnp.where(lane == c, squares, column[...])
-        return _
-
-    lax.fori_loop(0, chunks, join, 0)
+
+    steps(chunks, join)
     power[...] = jnp.transpose(column[...])[: power.shape[0]]
 
     def spread(d):

time: 19.7 us -> 19.5 us (0.990)
  no operation moved by 1% of the time
where the time goes in v2:
time: 19.5 us; the launch traced here: 19.4 us
  Pallas kernels  18.4 us (94%)
  local copies, waits for them, and re-layouts  0.97 us (5%)
    pallas_call x1, Pallas kernels, local(): pl.pallas_call(functools.partial(kernel, batch, span, times, chans, posit...  18.4 us
    unnamed x1, local copies, waits for them, and re-layouts  0.97 us

profile of v2, /device:TPU:0, one launch (start us, length us, event | category | flops | bytes accessed | tf_op | source)
XLA Modules:
  0.0 19.4 jit_solution(1270150514098910614)
XLA Ops:
  0.0 18.4 %shard_map.46 = bf16[8,256,256]{2,1,0:T(8,128)(2,1)S(1)} custom-call(f32[8,256,256]{2,1,0:T(8,128)} %bitcast.6, bf16[8,256,256]{2,1,0:T(8,128)(2,1)} %bitcast.7, bf16[8,256,256]{2,1,0:T(8,128)(2,1)} %bitcast.8, f32[1,256]{1,0:T(1,128)} %bitcast.9), custom_call_target="tpu_custom_call" | custom-call | tf_op jit(solution)/shard_map/pallas_call | solution.py:193
  18.4 1.0 %copy.6 = bf16[2,1024,256]{2,1,0:T(8,128)(2,1)} copy(bf16[2,1024,256]{2,1,0:T(8,128)(2,1)S(1)} %bitcast.5) | data formatting | bytes 2097152
